TPU v7x, 32 devices: a whole 2x2x4 slice. The times are simulated.
32 devices in a mesh: groups: 2 (over x), expert: 16 (over z, y, core).
Axes of the slice: x: 2, y: 2, z: 4, core: 2. Of those that a mesh axis runs over, the one named last changes fastest.
Arguments:
- query_features: bfloat16 [4096, 1024], P(('groups', 'expert')), parts along dimension 0, may hold values from -6 to 6
- query_job_label: int32 [4096], P(('groups', 'expert')), parts along dimension 0, may hold values from 0 to 7, as said below
- selected_specialists: int32 [4096, 2], P(('groups', 'expert')), parts along dimension 0, may hold values from 0 to 8, as said below
- whole_number_mixing_factors: int32 [4096, 2], P(('groups', 'expert')), parts along dimension 0, may hold values from 1 to 8
- copy_room_sizes: int32 [16], replicated, may hold values from 256 to 384, as said below
- first_layer_matrix: bfloat16 [16, 1024, 2048], P('expert'), as said below
- second_layer_matrix: bfloat16 [16, 2048, 1024], P('expert'), as said below
Outputs:
- mixture: bfloat16 [4096, 1024], P(('groups', 'expert')), parts along dimension 0
There are 2 independent parts, one for each index of `groups`. A program takes and returns all parts, laid end to end along the dimension named above; an argument that names none is the same for every part. Nothing has to cross between parts.
Inputs may be any that keep to these rules, and one draw needn't show every extreme that they name: `query_job_label`: each request's task number; column 0 of `selected_specialists` names a task expert of this task. `selected_specialists`: column 0 names a task expert of the row's task (number r from 8 on is task expert r - 8), column 1 a shared expert (below 8). From the rows of one device at most 32 entries go to one expert copy, and in every draw some copy receives exactly 32 entries from every device. `copy_room_sizes`: some copy has capacity 384 and some copy 2 * 128. `first_layer_matrix`: the 1 copies of one shared expert hold equal weights. `second_layer_matrix`: the 1 copies of one shared expert hold equal weights.
All inputs are finite; a program needn't handle non-finite values.
Results may differ from a plain program's by a relative error of at most 0.0058.
Values may be sent and summed in bfloat16 or wider, within the bound.
A program may use at most 64 MiB of HBM per device.

v0:
```python
import functools

import jax
import jax.numpy as jnp
from jax import lax
from jax.experimental import pallas as pl
from jax.experimental.pallas import tpu as pltpu
from jax.sharding import PartitionSpec as P

TASKS = 8
SHARED = 8
MESH = pl.DeviceIdType.MESH
CHUNKS = 4


def flip(a, b, n):
    total, bit = 0, 1
    while bit < n:
        x, y = (a // bit) % 2, (b // bit) % 2
        total = total + bit * (x + y - 2 * x * y)
        bit *= 2
    return total


def each(lo, hi, fn):
    if hi - lo <= 16:
        for d in range(lo, hi):
            fn(d)
    else:

        @pl.loop(lo, hi)
        def _(d):
            fn(d)


def kernel(
    n,
    slot,
    chunks,
    room_ref,
    label_ref,
    sel_ref,
    mix_ref,
    x_ref,
    w1_hbm,
    w2_hbm,
    out_ref,
    w1,
    w2,
    guests,
    outgoing,
    inbox,
    hidden,
    results,
    returned,
    home_out,
    home_in,
    partial,
    counts,
    route,
    w_sem,
    dense_sem,
    back_sem,
    route_sem,
    tally_send,
    tally_recv,
    near_send,
    near_recv,
    far_send,
    far_recv,
    near_rsend,
    near_rrecv,
    far_rsend,
    far_rrecv,
):
    me = lax.axis_index("expert")
    group = lax.axis_index("groups")
    half = n // 2
    rows, width = x_ref.shape
    span = half * slot
    part = width // chunks
    hid = w1.shape[1]
    padded = counts.shape[2]
    copies, task_width = n // (2 * SHARED), n // (2 * TASKS)

    load1 = pltpu.make_async_copy(w1_hbm.at[0], w1, w_sem.at[0])
    load2 = pltpu.make_async_copy(w2_hbm.at[0], w2, w_sem.at[1])
    load1.start()
    load2.start()

    barrier = pltpu.get_barrier_semaphore()

    def peer(d):
        return (group, flip(me, d, n))

    each(
        1,
        n,
        lambda d: pl.semaphore_signal(
            barrier, inc=1, device_id=peer(d), device_id_type=MESH
        ),
    )

    def remote(src, dst, send, recv, d):
        return pltpu.make_async_remote_copy(
            src_ref=src,
            dst_ref=dst,
            send_sem=send,
            recv_sem=recv,
            device_id=peer(d),
            device_id_type=MESH,
        )

    def block(first, d, k=None):
        start = first + d * slot
        if not isinstance(d, int):
            start = pl.multiple_of(start, slot)
        if k is None:
            return (pl.ds(start, slot), slice(None))
        return (pl.ds(start, slot), pl.ds(k * part, part))

    def columns(k):
        return (slice(None), pl.ds(k * part, part))

    def tally(d):
        return remote(
            counts.at[0], counts.at[d], tally_send.at[d], tally_recv.at[d], d
        )

    def plan():
        return remote(route.at[0], route.at[1], route_sem.at[0], route_sem.at[1], half)

    def dense(k):
        return remote(
            x_ref.at[columns(k)],
            guests.at[columns(k)],
            dense_sem.at[0, k],
            dense_sem.at[1, k],
            half,
        )

    def back(k):
        return remote(
            home_out.at[columns(k)],
            home_in.at[columns(k)],
            back_sem.at[0, k],
            back_sem.at[1, k],
            half,
        )

    def near_dispatch(d):
        at = block(0, d)
        return remote(outgoing.at[at], inbox.at[at], near_send.at[d], near_recv.at[d], d)

    def far_dispatch(d, k):
        at = block(span, d, k)
        return remote(
            outgoing.at[at], inbox.at[at], far_send.at[d, k], far_recv.at[d, k], d
        )

    def near_answer(d):
        at = block(0, d)
        return remote(
            results.at[at], returned.at[at], near_rsend.at[d], near_rrecv.at[d], d
        )

    def far_answer(d, k):
        at = block(span, d, k)
        return remote(
            results.at[at], returned.at[at], far_rsend.at[d, k], far_rrecv.at[d, k], d
        )

    lane = lax.broadcasted_iota(jnp.int32, (1, rows), 1)
    task_id = SHARED * copies + label_ref[...] * task_width + sel_ref[0:1, :] - SHARED
    shared_id = sel_ref[1:2, :] * copies + lane % copies
    expert = lax.broadcasted_iota(jnp.int32, (padded, rows), 0)
    task_hot = (expert == task_id).astype(jnp.float32)
    shared_hot = (expert == shared_id).astype(jnp.float32)
    hot = (task_hot + shared_hot).astype(jnp.bfloat16)
    earlier = (
        lax.broadcasted_iota(jnp.int32, (rows, rows), 0)
        < lax.broadcasted_iota(jnp.int32, (rows, rows), 1)
    ).astype(jnp.float32)
    before = jnp.dot(
        hot, earlier.astype(jnp.bfloat16), preferred_element_type=jnp.float32
    )
    task_rank = jnp.sum(before * task_hot, axis=0, keepdims=True)
    shared_rank = jnp.sum(before * shared_hot, axis=0, keepdims=True)
    counts[0] = lax.dot_general(
        jnp.ones((8, rows), jnp.bfloat16),
        hot,
        (((1,), (1,)), ((), ())),
        preferred_element_type=jnp.float32,
    )[:1]

    task_slot = (task_id ^ me) * slot + task_rank.astype(jnp.int32)
    shared_slot = (shared_id ^ me) * slot + shared_rank.astype(jnp.int32)
    task_near = task_slot < span
    near_slot = jnp.where(task_near, task_slot, shared_slot)
    far_slot = jnp.where(task_near, shared_slot, task_slot) - span
    route[0] = far_slot
    slot_row = lax.broadcasted_iota(jnp.int32, (span, rows), 0)

    def choice(slots):
        return (slot_row == slots).astype(jnp.float32).astype(jnp.bfloat16)

    def pack(chosen, block_rows):
        return jnp.dot(chosen, block_rows, preferred_element_type=jnp.float32).astype(
            jnp.bfloat16
        )

    near_pack = pack(choice(near_slot), x_ref[...])
    outgoing[pl.ds(0, span)] = near_pack
    inbox[pl.ds(0, slot)] = near_pack[:slot]

    pl.semaphore_wait(barrier, n - 1)
    plan().start()
    for k in range(chunks):
        dense(k).start()
    each(1, n, lambda d: tally(d).start())
    each(1, half, lambda d: near_dispatch(d).start())

    plan().wait_recv()
    guest_slot = route[1]
    guest_choice = choice(guest_slot)
    for k in range(chunks):
        dense(k).wait_recv()
        packed = pack(guest_choice, guests[columns(k)])
        outgoing[pl.ds(span, span), pl.ds(k * part, part)] = packed
        inbox[pl.ds(span, slot), pl.ds(k * part, part)] = packed[:slot]
        each(1, half, lambda d: far_dispatch(d, k).start())

    tile = min(512, hid)

    def expand(first):
        @pl.loop(0, hid // tile)
        def _(t):
            cols = pl.ds(pl.multiple_of(t * tile, tile), tile)
            h = jnp.dot(
                inbox[pl.ds(first, span)],
                w1[:, cols],
                preferred_element_type=jnp.float32,
            )
            hidden[:, cols] = jax.nn.gelu(h).astype(jnp.bfloat16)

    def shrink(first, cols):
        y = jnp.dot(hidden[...], w2[:, cols], preferred_element_type=jnp.float32)
        results[pl.ds(first, span), cols] = y.astype(jnp.bfloat16)

    load1.wait()
    load2.wait()
    each(1, half, lambda d: near_dispatch(d).wait_recv())
    expand(0)

    out_tile = min(512, width)

    @pl.loop(0, width // out_tile)
    def _(t):
        shrink(0, pl.ds(pl.multiple_of(t * out_tile, out_tile), out_tile))

    each(1, half, lambda d: near_answer(d).start())
    returned[pl.ds(0, slot)] = results[pl.ds(0, slot)]

    for k in range(chunks):
        each(1, half, lambda d: far_dispatch(d, k).wait_recv())
    expand(span)
    for k in range(chunks):
        shrink(span, pl.ds(k * part, part))
        each(1, half, lambda d: far_answer(d, k).start())
        own = (pl.ds(span, slot), pl.ds(k * part, part))
        returned[own] = results[own]

    each(1, n, lambda d: tally(d).wait_recv())

    def column(row):
        return jnp.broadcast_to(row, (128, row.shape[1])).T[:, :1]

    offset = jnp.zeros((1, padded), jnp.float32)
    for d in range(1, n):
        offset = offset + counts[d] * jnp.where(flip(me, d, n) < me, 1.0, 0.0)
    offset = column(offset)
    arrival_task = task_rank + jnp.sum(task_hot * offset, axis=0, keepdims=True)
    arrival_shared = shared_rank + jnp.sum(shared_hot * offset, axis=0, keepdims=True)
    room_task = jnp.zeros((1, rows), jnp.int32)
    room_shared = jnp.zeros((1, rows), jnp.int32)
    for e in range(n):
        size = room_ref[e]
        if e < half:
            room_shared = jnp.where(shared_id == e, size, room_shared)
        else:
            room_task = jnp.where(task_id == e, size, room_task)
    keep_task = (arrival_task < room_task.astype(jnp.float32)).astype(jnp.float32)
    keep_shared = (arrival_shared < room_shared.astype(jnp.float32)).astype(jnp.float32)
    mix = mix_ref[...].astype(jnp.float32)
    total = mix[0:1] + mix[1:2]
    task_weight = mix[0:1] / total * keep_task
    shared_weight = mix[1:2] / total * keep_shared
    near_weight = column(jnp.where(task_near, task_weight, shared_weight))
    far_weight = column(jnp.where(task_near, shared_weight, task_weight))
    slot_lane = lax.broadcasted_iota(jnp.int32, (rows, span), 1).astype(jnp.float32)

    def reader(slots):
        slots = column(slots.astype(jnp.float32))
        return (slot_lane == slots).astype(jnp.float32).astype(jnp.bfloat16)

    near_reader = reader(near_slot)
    guest_reader = reader(guest_slot)

    each(1, half, lambda d: near_answer(d).wait_recv())
    partial[...] = (
        jnp.dot(
            near_reader, returned[pl.ds(0, span)], preferred_element_type=jnp.float32
        )
        * near_weight
    )

    for k in range(chunks):
        each(1, half, lambda d: far_answer(d, k).wait_recv())
        home_out[columns(k)] = pack(
            guest_reader, returned[pl.ds(span, span), pl.ds(k * part, part)]
        )
        back(k).start()

    for k in range(chunks):
        back(k).wait_recv()
        out_ref[columns(k)] = (
            partial[columns(k)] + home_in[columns(k)].astype(jnp.float32) * far_weight
        ).astype(jnp.bfloat16)

    plan().wait_send()
    each(1, n, lambda d: tally(d).wait_send())
    for k in range(chunks):
        dense(k).wait_send()
        back(k).wait_send()

    def drain(d):
        near_dispatch(d).wait_send()
        near_answer(d).wait_send()
        for k in range(chunks):
            far_dispatch(d, k).wait_send()
            far_answer(d, k).wait_send()

    each(1, half, drain)


def solution(mesh):
    n = mesh.shape["expert"]

    def shards(x, label, sel, mix, room, first, second):
        rows, width = x.shape
        hid = first.shape[2]
        slot = -(-(4 * rows // n) // 16) * 16
        chunks = CHUNKS
        half = n // 2
        padded = -(-n // 128) * 128
        flat = pltpu.VMEM((n * slot, width), jnp.bfloat16)
        plain = pltpu.VMEM((rows, width), jnp.bfloat16)
        vmem = pl.BlockSpec(memory_space=pltpu.VMEM)
        anywhere = pl.BlockSpec(memory_space=pl.ANY)
        dma = pltpu.SemaphoreType.DMA
        return pl.pallas_call(
            functools.partial(kernel, n, slot, chunks),
            out_shape=jax.ShapeDtypeStruct((rows, width), jnp.bfloat16),
            in_specs=[pl.BlockSpec(memory_space=pltpu.SMEM)]
            + [vmem] * 4
            + [anywhere] * 2,
            out_specs=vmem,
            scratch_shapes=[
                pltpu.VMEM(first.shape[1:], jnp.bfloat16),
                pltpu.VMEM(second.shape[1:], jnp.bfloat16),
                plain,
                flat,
                flat,
                pltpu.VMEM((half * slot, hid), jnp.bfloat16),
                flat,
                flat,
                plain,
                plain,
                pltpu.VMEM((rows, width), jnp.float32),
                pltpu.VMEM((n, 1, padded), jnp.float32),
                pltpu.VMEM((2, 1, rows), jnp.int32),
                dma((2,)),
                dma((2, chunks)),
                dma((2, chunks)),
                dma((2,)),
                dma((n,)),
                dma((n,)),
                dma((half,)),
                dma((half,)),
                dma((half, chunks)),
                dma((half, chunks)),
                dma((half,)),
                dma((half,)),
                dma((half, chunks)),
                dma((half, chunks)),
            ],
            compiler_params=pltpu.CompilerParams(
                collective_id=0, has_side_effects=True
            ),
        )(room, label.reshape(1, rows), sel.T, mix.T, x, first, second)

    in_specs = (
        P(("groups", "expert"), None),
        P(("groups", "expert")),
        P(("groups", "expert"), None),
        P(("groups", "expert"), None),
        P(),
        P("expert", None, None),
        P("expert", None, None),
    )
    return jax.shard_map(
        shards,
        mesh=mesh,
        in_specs=in_specs,
        out_specs=P(("groups", "expert"), None),
        check_vma=False,
    )
```

profile of v0, /device:TPU:0, one launch (start us, length us, event | category | flops | bytes accessed | tf_op | source)
XLA Modules:
  0.0 51.6 jit_solution(4690028285739517586)
XLA Ops:
  0.0 50.0 %shard_map.73 = bf16[128,1024]{1,0:T(8,128)(2,1)} custom-call(s32[16]{0:T(128)} %room_ref.1, s32[1,128]{1,0:T(1,128)} %bitcast.5, s32[2,128]{1,0:T(2,128)} %bitcast.3, s32[2,128]{1,0:T(2,128)} %bitcast.4, bf16[128,1024]{1,0:T(8,128)(2,1)} %x_ref.1, bf16[1,1024,2048]{2,1,0:T(8,128)(2,1)} %w1_hbm.1, bf16[1,2048,1024]{2,1,0:T(8,128)(2,1)} %w2_hbm.1), custom_call_target="tpu_custom_call" | custom-call | tf_op jit(solution)/shard_map/pallas_call | solution.py:361
  50.0 1.7 %copy.9 = bf16[128,1024]{1,0:T(8,128)(2,1)} copy(bf16[128,1024]{1,0:T(8,128)(2,1)} %shard_map.73) | data formatting | bytes 524288
where the time goes:
time: 51.8 us; the launch traced here: 51.6 us
  Pallas kernels  50 us (97%)
  local copies, waits for them, and re-layouts  1.67 us (3%)
    pallas_call x1, Pallas kernels, shards(): pl.pallas_call(functools.partial(kernel, n, slot, chunks), out_shape=jax....  50 us
    unnamed x1, local copies, waits for them, and re-layouts  1.67 us

commit v1 on v0

v1 whole, which is shorter than its diff:
```python
import functools

import jax
import jax.numpy as jnp
from jax import lax
from jax.experimental import pallas as pl
from jax.experimental.pallas import tpu as pltpu
from jax.sharding import PartitionSpec as P

TASKS = 8
SHARED = 8
MESH = pl.DeviceIdType.MESH
CHUNKS = 4
FERRIED = ()
OUTER = ('own', 'reply', 'other', 'weigh', 'far0', 'far1')
INNER = ('guest0', 'guest1', 'far0', 'lodge', 'weigh', 'far1', 'back0', 'own', 'reply', 'back1')
LIMIT = 56 * 2**20


def flip(a, b, n):
    total, bit = 0, 1
    while bit < n:
        x, y = (a // bit) % 2, (b // bit) % 2
        total = total + bit * (x + y - 2 * x * y)
        bit *= 2
    return total


def each(lo, hi, fn):
    if hi - lo <= 16:
        for d in range(lo, hi):
            fn(d)
    else:

        @pl.loop(lo, hi)
        def _(d):
            fn(d)


def kernel(
    n,
    slot,
    chunks,
    room_ref,
    label_hbm,
    sel_hbm,
    mix_hbm,
    x_hbm,
    w1_hbm,
    w2_hbm,
    out_hbm,
    label_ref,
    sel_ref,
    mix_ref,
    x_ref,
    out_ref,
    w1,
    w2,
    visits,
    outgoing,
    relayed,
    inbox,
    hidden,
    results,
    returned,
    relay_in,
    home_out,
    home_in,
    partial,
    weights,
    counts,
    route_out,
    route_in,
    transit,
    w_sem,
    in_sem,
    out_sem,
    dense_send,
    pass_send,
    visit_recv,
    route_send,
    route_recv,
    tally_send,
    tally_recv,
    near_send,
    near_recv,
    lodge_send,
    lodge_recv,
    far_send,
    far_recv,
    near_rsend,
    near_rrecv,
    far_rsend,
    far_rrecv,
    back_send,
    back_recv,
    shut_send,
    shut_recv,
):
    me = lax.axis_index("expert")
    group = lax.axis_index("groups")
    lanes = n // 4
    half = 2 * lanes
    mirror = 3 * lanes
    rows, width = x_hbm.shape
    span = half * slot
    cross = lanes // 2
    block = lanes * slot
    part = width // chunks
    hid = w1.shape[1]
    padded = counts.shape[2]
    copies, task_width = n // (2 * SHARED), n // (2 * TASKS)
    plane = me // lanes
    inner = plane // 2 + plane % 2 == 1
    outer = plane // 2 + plane % 2 != 1

    barrier = pltpu.get_barrier_semaphore()

    def peer(d):
        return (group, flip(me, d, n))

    each(
        1,
        n,
        lambda d: pl.semaphore_signal(
            barrier, inc=1, device_id=peer(d), device_id_type=MESH
        ),
    )

    inputs = [
        pltpu.make_async_copy(src, dst, in_sem.at[i])
        for i, (src, dst) in enumerate(
            (
                (label_hbm, label_ref),
                (sel_hbm, sel_ref),
                (mix_hbm, mix_ref),
                (x_hbm, x_ref),
            )
        )
    ]
    for load in inputs:
        load.start()
    load1 = pltpu.make_async_copy(w1_hbm.at[0], w1, w_sem.at[0])
    load2 = pltpu.make_async_copy(w2_hbm.at[0], w2, w_sem.at[1])
    load1.start()
    load2.start()

    def remote(src, dst, send, recv, d):
        return pltpu.make_async_remote_copy(
            src_ref=src,
            dst_ref=dst,
            send_sem=send,
            recv_sem=recv,
            device_id=peer(d),
            device_id_type=MESH,
        )

    def at(first, d, k=None):
        start = first + d * slot
        if not isinstance(start, int):
            start = pl.multiple_of(start, slot)
        if k is None:
            return (pl.ds(start, slot), slice(None))
        return (pl.ds(start, slot), pl.ds(k * part, part))

    def columns(k):
        return (slice(None), pl.ds(k * part, part))

    def tally(d):
        return remote(counts.at[0], counts.at[d], tally_send, tally_recv, d)

    def route(i, j, d):
        return remote(
            route_out.at[i], route_in.at[j], route_send.at[i], route_recv.at[j], d
        )

    def dense(j, d, k):
        return remote(
            x_ref.at[columns(k)],
            visits.at[(j,) + columns(k)],
            dense_send,
            visit_recv.at[j, k],
            d,
        )

    def pass_on(k):
        return remote(
            visits.at[(2,) + columns(k)],
            visits.at[(1,) + columns(k)],
            pass_send,
            visit_recv.at[1, k],
            mirror,
        )

    def near(side, l):
        d = side * lanes + l
        return remote(
            outgoing.at[at(0, d)],
            inbox.at[at(0, d)],
            near_send,
            near_recv.at[side],
            d,
        )

    def lodge(l, k):
        return remote(
            relayed.at[(2,) + at(0, l, k)],
            inbox.at[at(block, l, k)],
            lodge_send,
            lodge_recv,
            l,
        )

    def far(g, side, l, k):
        d = side * lanes + l
        return remote(
            relayed.at[(g,) + at(0, d, k)],
            inbox.at[at((2 + g) * block, l, k)],
            far_send.at[g],
            far_recv.at[g],
            d,
        )

    def near_answer(d):
        return remote(
            results.at[at(0, d)], returned.at[at(0, d)], near_rsend, near_rrecv, d
        )

    def far_answer(g, side, l, k):
        d = side * lanes + l
        return remote(
            results.at[at((2 + g) * block, l, k)],
            relay_in.at[(g,) + at(0, d, k)],
            far_rsend.at[g],
            far_rrecv.at[g, k],
            d,
        )

    def shuttle(g, l, k):
        return remote(
            results.at[at((1 + g) * block, l, k)],
            transit.at[(g,) + at(0, l, k)],
            shut_send.at[g],
            shut_recv.at[g, k],
            l,
        )

    def ferry(g, l, k):
        if g == 0:
            dst, send, recv = returned.at[at(block, l, k)], near_rsend, near_rrecv
        else:
            dst = relay_in.at[(g - 1,) + at(block, l, k)]
            send, recv = far_rsend.at[g - 1], far_rrecv.at[g - 1, k]
        return remote(transit.at[(g,) + at(0, l, k)], dst, send, recv, lanes)

    def back(g, k):
        return remote(
            home_out.at[(g,) + columns(k)],
            home_in.at[columns(k)],
            back_send,
            back_recv.at[k],
            mirror if g == 0 else half,
        )

    def put(k):
        return pltpu.make_async_copy(
            out_ref.at[columns(k)], out_hbm.at[columns(k)], out_sem.at[k]
        )

    def bulk(sem, count, k=None):
        area = inbox.at[pl.ds(0, count * slot)]
        if k is not None:
            area = inbox.at[(pl.ds(0, count * slot), pl.ds(k * part, part))]
        return pltpu.make_async_copy(area, area, sem)

    for load in inputs:
        load.wait()
    lane = lax.broadcasted_iota(jnp.int32, (1, rows), 1)
    task_id = SHARED * copies + label_ref[...] * task_width + sel_ref[0:1, :] - SHARED
    shared_id = sel_ref[1:2, :] * copies + lane % copies
    expert = lax.broadcasted_iota(jnp.int32, (padded, rows), 0)
    task_hot = (expert == task_id).astype(jnp.float32)
    shared_hot = (expert == shared_id).astype(jnp.float32)
    hot = (task_hot + shared_hot).astype(jnp.bfloat16)
    earlier = (
        lax.broadcasted_iota(jnp.int32, (rows, rows), 0)
        < lax.broadcasted_iota(jnp.int32, (rows, rows), 1)
    ).astype(jnp.float32)
    before = jnp.dot(
        hot, earlier.astype(jnp.bfloat16), preferred_element_type=jnp.float32
    )
    task_rank = jnp.sum(before * task_hot, axis=0, keepdims=True)
    shared_rank = jnp.sum(before * shared_hot, axis=0, keepdims=True)
    counts[0] = lax.dot_general(
        jnp.ones((8, rows), jnp.bfloat16),
        hot,
        (((1,), (1,)), ((), ())),
        preferred_element_type=jnp.float32,
    )[:1]

    task_near = (task_id ^ me) < half
    near_id = jnp.where(task_near, task_id, shared_id)
    far_id = jnp.where(task_near, shared_id, task_id)
    near_rank = jnp.where(task_near, task_rank, shared_rank).astype(jnp.int32)
    far_rank = jnp.where(task_near, shared_rank, task_rank).astype(jnp.int32)
    near_slot = (near_id ^ me) * slot + near_rank
    relay = flip(me, half, n) * (1 - inner.astype(jnp.int32)) + flip(
        me, mirror, n
    ) * inner.astype(jnp.int32)
    route_out[0] = (far_id ^ relay) * slot + far_rank
    route_out[1] = (near_id ^ flip(me, lanes, n)) * slot + near_rank

    def choice(slots, count):
        slot_row = lax.broadcasted_iota(jnp.int32, (count, rows), 0)
        return (slot_row == slots).astype(jnp.float32).astype(jnp.bfloat16)

    def pack(chosen, block_rows):
        return jnp.dot(chosen, block_rows, preferred_element_type=jnp.float32).astype(
            jnp.bfloat16
        )

    near_pack = pack(choice(near_slot, span), x_ref[...])
    outgoing[...] = near_pack
    inbox[pl.ds(0, slot)] = near_pack[:slot]

    tile = min(1024, hid)
    out_tile = min(512, width)

    def expand(g):
        @pl.loop(0, hid // tile)
        def _(t):
            cols = pl.ds(pl.multiple_of(t * tile, tile), tile)
            h = jnp.dot(
                inbox[pl.ds(g * block, block)],
                w1[:, cols],
                preferred_element_type=jnp.float32,
            )
            hidden[:, cols] = jax.nn.gelu(h).astype(jnp.bfloat16)

    def shrink(g, cols):
        y = jnp.dot(hidden[...], w2[:, cols], preferred_element_type=jnp.float32)
        results[pl.ds(g * block, block), cols] = y.astype(jnp.bfloat16)

    def near_work(g):
        expand(g)

        @pl.loop(0, width // out_tile)
        def _(t):
            shrink(g, pl.ds(pl.multiple_of(t * out_tile, out_tile), out_tile))

        if g == 0:
            returned[pl.ds(0, slot)] = results[pl.ds(0, slot)]

    def far_work(g, send):
        with jax.named_scope(f'far_expand{g}'):
            expand(2 + g)
        with jax.named_scope(f'far_shrink{g}'):
            pair = min(2, chunks)
            for j in range(chunks // pair):
                shrink(2 + g, pl.ds(j * pair * part, pair * part))
                for k in range(j * pair, (j + 1) * pair):
                    send(k)

    def ferry_all(g):
        for k in range(chunks):
            bulk(shut_recv.at[g, k], lanes - cross, k).wait()
            each(cross, lanes, lambda l: ferry(g, l, k).start())

    def column(row):
        return jnp.broadcast_to(row, (128, row.shape[1])).T[:, :1]

    def reader(slots):
        slot_lane = lax.broadcasted_iota(jnp.int32, (rows, span), 1).astype(jnp.float32)
        slots = column(slots.astype(jnp.float32))
        return (slot_lane == slots).astype(jnp.float32).astype(jnp.bfloat16)

    def weigh():
        pltpu.make_async_copy(counts.at[pl.ds(1, n - 1)], counts.at[pl.ds(1, n - 1)], tally_recv).wait()
        offset = jnp.zeros((1, padded), jnp.float32)
        for d in range(1, n):
            offset = offset + counts[d] * jnp.where(flip(me, d, n) < me, 1.0, 0.0)
        offset = column(offset)
        arrival_task = task_rank + jnp.sum(task_hot * offset, axis=0, keepdims=True)
        arrival_shared = shared_rank + jnp.sum(
            shared_hot * offset, axis=0, keepdims=True
        )
        room_task = jnp.zeros((1, rows), jnp.int32)
        room_shared = jnp.zeros((1, rows), jnp.int32)
        for e in range(n):
            size = room_ref[e]
            if e < half:
                room_shared = jnp.where(shared_id == e, size, room_shared)
            else:
                room_task = jnp.where(task_id == e, size, room_task)
        keep_task = (arrival_task < room_task.astype(jnp.float32)).astype(jnp.float32)
        keep_shared = (arrival_shared < room_shared.astype(jnp.float32)).astype(
            jnp.float32
        )
        mix = mix_ref[...].astype(jnp.float32)
        total = mix[0:1] + mix[1:2]
        task_weight = mix[0:1] / total * keep_task
        shared_weight = mix[1:2] / total * keep_shared
        weights[0] = column(jnp.where(task_near, task_weight, shared_weight))
        weights[1] = column(jnp.where(task_near, shared_weight, task_weight))

    with jax.named_scope('barrier'):
        pl.semaphore_wait(barrier, n - 1)

    @pl.when(outer)
    def _():
        for k in range(chunks):
            dense(2, lanes, k).start()
            if k == 0:
                route(1, 2, lanes).start()
                route(0, 1, half).start()
        each(1, lanes, lambda l: near(0, l).start())
        each(1, n, lambda d: tally(d).start())

        def own():
            with jax.named_scope('o_wait_own'):
                load1.wait()
                load2.wait()
                bulk(near_recv.at[0], lanes - 1).wait()
            with jax.named_scope('o_work0'):
                near_work(0)

        def reply():
            each(1, lanes, lambda d: near_answer(d).start())

        def other():
            with jax.named_scope('o_wait_other'):
                bulk(near_recv.at[1], lanes).wait()
            with jax.named_scope('o_work1'):
                near_work(1)
            if 0 in FERRIED:
                for k in range(chunks):
                    each(cross, lanes, lambda l: shuttle(0, l, k).start())
                each(0, cross, lambda l: near_answer(lanes + l).start())
            else:
                each(lanes, half, lambda d: near_answer(d).start())

        def await_far(g):
            with jax.named_scope(f'o_far_wait{g}'):
                bulk(far_recv.at[g], lanes).wait()

        def far_step(g):
            def send(k):
                if 1 + g in FERRIED:
                    each(cross, lanes, lambda l: shuttle(1 + g, l, k).start())
                    each(0, cross, lambda l: far_answer(g, 1, l, k).start())
                else:
                    each(0, lanes, lambda l: far_answer(g, 1, l, k).start())

            far_work(g, send)

        def carry(g):
            with jax.named_scope(f'o_ferry{g}'):
                ferry_all(g)

        def weigh_step():
            with jax.named_scope('o_weigh'):
                weigh()

        steps = {"own": own, "reply": reply, "other": other, "weigh": weigh_step}
        for g in range(2):
            steps[f"await{g}"] = functools.partial(await_far, g)
            steps[f"far{g}"] = functools.partial(far_step, g)
        for g in range(3):
            steps[f"ferry{g}"] = functools.partial(carry, g)
        if "await1" not in OUTER:
            steps["far1"] = lambda: (await_far(1), far_step(1))
        steps["far0"] = lambda: (await_far(0), far_step(0))
        for step in OUTER:
            steps[step]()

    @pl.when(inner)
    def _():
        for k in range(chunks):
            dense(0, mirror, k).start()
            if k == 0:
                route(0, 0, mirror).start()
        each(0, lanes, lambda l: near(1, l).start())
        each(1, lanes, lambda l: near(0, l).start())
        each(1, n, lambda d: tally(d).start())

        def host(g, chosen, k):
            packed = pack(chosen, visits[(g,) + columns(k)])
            relayed[(g, slice(None), pl.ds(k * part, part))] = packed
            inbox[at((2 + g) * block, 0, k)] = packed[:slot]
            each(1, lanes, lambda l: far(g, 0, l, k).start())
            each(0, lanes, lambda l: far(g, 1, l, k).start())

        def guest0():
            route(1, 2, lanes).wait_recv()
            route(0, 0, mirror).wait_recv()
            lodge_choice = choice(route_in[2], block)
            guest_choice = choice(route_in[0], span)
            for k in range(chunks):
                with jax.named_scope(f'i_waitG{k}'):
                    dense(2, lanes, k).wait_recv()
                pass_on(k).start()
                with jax.named_scope(f'i_waitg0_{k}'):
                    dense(0, mirror, k).wait_recv()
                with jax.named_scope(f'i_host0_{k}'):
                    host(0, guest_choice, k)
                packed = pack(lodge_choice, visits[(2,) + columns(k)])
                relayed[(2, pl.ds(0, block), pl.ds(k * part, part))] = packed
                inbox[at(block, 0, k)] = packed[:slot]
                each(1, lanes, lambda l: lodge(l, k).start())
            load1.wait()
            load2.wait()

        def own():
            with jax.named_scope('i_wait_own'):
                bulk(near_recv.at[0], lanes - 1).wait()
            with jax.named_scope('i_work0'):
                near_work(0)

        def reply():
            each(1, lanes, lambda d: near_answer(d).start())

        def guest1():
            route(0, 1, half).wait_recv()
            guest_choice = choice(route_in[1], span)
            for k in range(chunks):
                with jax.named_scope(f'i_waitg1_{k}'):
                    pass_on(k).wait_recv()
                with jax.named_scope(f'i_host1_{k}'):
                    host(1, guest_choice, k)

        def lodged():
            with jax.named_scope('i_waitlodge'):
                bulk(lodge_recv, lanes - 1).wait()
            with jax.named_scope('i_work1'):
                near_work(1)
            each(lanes, half, lambda d: near_answer(d).start())

        def take_back(g, lo, hi):
            guest_reader = reader(route_in[g])
            for k in range(lo, hi):
                with jax.named_scope(f'i_waitans{g}_{k}'):
                    bulk(far_rrecv.at[g, k], half - 1, k).wait()
                home_out[(g,) + columns(k)] = pack(
                    guest_reader, relay_in[(g, slice(None), pl.ds(k * part, part))]
                )
                back(g, k).start()

        def far_step(g):
            def send(k):
                each(1, lanes, lambda l: far_answer(g, 0, l, k).start())
                relay_in[(g,) + at(0, 0, k)] = results[at((2 + g) * block, 0, k)]

            with jax.named_scope(f'i_far_wait{g}'):
                bulk(far_recv.at[g], lanes - 1).wait()
            far_work(g, send)

        def weigh_step():
            with jax.named_scope('i_weigh'):
                weigh()

        steps = {"own": own, "reply": reply, "guest0": guest0, "guest1": guest1, "lodge": lodged, "weigh": weigh_step}
        for g in range(2):
            steps[f"far{g}"] = functools.partial(far_step, g)
            steps[f"back{g}"] = functools.partial(take_back, g, 0, chunks)
            steps[f"back{g}a"] = functools.partial(take_back, g, 0, chunks // 2)
            steps[f"back{g}b"] = functools.partial(take_back, g, chunks // 2, chunks)
        for step in INNER:
            steps[step]()

    near_reader = reader(near_slot)
    with jax.named_scope('wait_near_ans'):
        bulk(near_rrecv, half - 1).wait()
    partial[...] = (
        jnp.dot(near_reader, returned[...], preferred_element_type=jnp.float32)
        * weights[0]
    )
    far_weight = weights[1]
    for k in range(chunks):
        with jax.named_scope(f'wait_back{k}'):
            back(0, k).wait_recv()
        out_ref[columns(k)] = (
            partial[columns(k)] + home_in[columns(k)].astype(jnp.float32) * far_weight
        ).astype(jnp.bfloat16)
        put(k).start()

    with jax.named_scope('drain'):
        pltpu.make_async_copy(
            counts.at[pl.ds(1, n - 1)], counts.at[pl.ds(1, n - 1)], tally_send
        ).wait()
        bulk(near_rsend, half - 1).wait()
        route(0, 0, mirror).wait_send()
        pltpu.make_async_copy(x_ref, home_in, dense_send).wait()

        @pl.when(outer)
        def _():
            route(1, 2, lanes).wait_send()
            bulk(near_send, lanes - 1).wait()
            for g in range(2):
                bulk(far_rsend.at[g], lanes).wait()
            for g in FERRIED:
                bulk(shut_send.at[g], lanes - cross).wait()

        @pl.when(inner)
        def _():
            bulk(near_send, half - 1).wait()
            pltpu.make_async_copy(x_ref, home_in, pass_send).wait()
            bulk(lodge_send, lanes - 1).wait()
            for g in range(2):
                bulk(far_send.at[g], half - 1).wait()
                bulk(far_rsend.at[g], lanes - 1).wait()
            pltpu.make_async_copy(home_out, home_out, back_send).wait()

        for k in range(chunks):
            put(k).wait()


def solution(mesh):
    n = mesh.shape["expert"]

    def shards(x, label, sel, mix, room, first, second):
        rows, width = x.shape
        hid = first.shape[2]
        slot = -(-(4 * rows // n) // 16) * 16
        lanes, half = n // 4, n // 2
        chunks = CHUNKS if lanes <= 8 else 1
        padded = -(-n // 128) * 128
        bf16, f32, i32 = jnp.bfloat16, jnp.float32, jnp.int32
        anywhere = pl.BlockSpec(memory_space=pltpu.HBM)
        dma = pltpu.SemaphoreType.DMA
        return pl.pallas_call(
            functools.partial(kernel, n, slot, chunks),
            out_shape=jax.ShapeDtypeStruct((rows, width), bf16),
            in_specs=[pl.BlockSpec(memory_space=pltpu.SMEM)]
            + [anywhere] * 6,
            out_specs=anywhere,
            scratch_shapes=[
                pltpu.VMEM((1, rows), i32),
                pltpu.VMEM((2, rows), i32),
                pltpu.VMEM((2, rows), i32),
                pltpu.VMEM((rows, width), bf16),
                pltpu.VMEM((rows, width), bf16),
                pltpu.VMEM(first.shape[1:], bf16),
                pltpu.VMEM(second.shape[1:], bf16),
                pltpu.VMEM((3, rows, width), bf16),
                pltpu.VMEM((half * slot, width), bf16),
                pltpu.VMEM((3, half * slot, width), bf16),
                pltpu.VMEM((n * slot, width), bf16),
                pltpu.VMEM((lanes * slot, hid), bf16),
                pltpu.VMEM((n * slot, width), bf16),
                pltpu.VMEM((half * slot, width), bf16),
                pltpu.VMEM((2, half * slot, width), bf16),
                pltpu.VMEM((2, rows, width), bf16),
                pltpu.VMEM((rows, width), bf16),
                pltpu.VMEM((rows, width), f32),
                pltpu.VMEM((2, rows, 1), f32),
                pltpu.VMEM((n, 1, padded), f32),
                pltpu.VMEM((2, 1, rows), i32),
                pltpu.VMEM((3, 1, rows), i32),
                pltpu.VMEM((3, lanes * slot, width), bf16),
                dma((2,)),
                dma((4,)),
                dma((chunks,)),
                dma(()),
                dma(()),
                dma((3, chunks)),
                dma((2,)),
                dma((3,)),
                dma(()),
                dma(()),
                dma(()),
                dma((2,)),
                dma(()),
                dma(()),
                dma((2,)),
                dma((2,)),
                dma(()),
                dma(()),
                dma((2,)),
                dma((2, chunks)),
                dma(()),
                dma((chunks,)),
                dma((3,)),
                dma((3, chunks)),
            ],
            compiler_params=pltpu.CompilerParams(
                collective_id=0, has_side_effects=True, vmem_limit_bytes=LIMIT
            ),
        )(room, label.reshape(1, rows), sel.T, mix.T, x, first, second)

    in_specs = (
        P(("groups", "expert"), None),
        P(("groups", "expert")),
        P(("groups", "expert"), None),
        P(("groups", "expert"), None),
        P(),
        P("expert", None, None),
        P("expert", None, None),
    )
    return jax.shard_map(
        shards,
        mesh=mesh,
        in_specs=in_specs,
        out_specs=P(("groups", "expert"), None),
        check_vma=False,
    )
```

time: 51.8 us -> 43.7 us (0.84)
  Pallas kernels: 50 us -> 41.8 us
    pallas_call x1, Pallas kernels: 50 us -> 41.8 us  [shards(): pl.pallas_call(functools.partial(kernel, n, slot, chunks), out_shape=jax....]
where the time goes in v1:
time: 43.7 us; the launch traced here: 43.5 us
  Pallas kernels  41.8 us (96%)
  local copies, waits for them, and re-layouts  1.67 us (4%)
    pallas_call x1, Pallas kernels, shards(): pl.pallas_call(functools.partial(kernel, n, slot, chunks), out_shape=jax....  41.8 us
    unnamed x1, local copies, waits for them, and re-layouts  1.67 us

profile of v1, /device:TPU:0, one launch (start us, length us, event | category | flops | bytes accessed | tf_op | source)
XLA Modules:
  0.0 43.5 jit_solution(15997214454420248996)
XLA Ops:
  0.0 41.8 %shard_map.73 = bf16[128,1024]{1,0:T(8,128)(2,1)} custom-call(s32[16]{0:T(128)} %room_ref.1, s32[1,128]{1,0:T(1,128)} %bitcast.5, s32[2,128]{1,0:T(2,128)} %bitcast.3, s32[2,128]{1,0:T(2,128)} %bitcast.4, bf16[128,1024]{1,0:T(8,128)(2,1)} %x_hbm.1, bf16[1,1024,2048]{2,1,0:T(8,128)(2,1)} %w1_hbm.1, bf16[1,2048,1024]{2,1,0:T(8,128)(2,1)} %w2_hbm.1), custom_call_target="tpu_custom_call" | custom-call | tf_op jit(solution)/shard_map/pallas_call | solution.py:630
  41.9 1.7 %copy.9 = bf16[128,1024]{1,0:T(8,128)(2,1)} copy(bf16[128,1024]{1,0:T(8,128)(2,1)} %shard_map.73) | data formatting | bytes 524288

commit v2 on v1

--- a/solution.py
+++ b/solution.py
@@ -11,9 +11,8 @@
 SHARED = 8
 MESH = pl.DeviceIdType.MESH
 CHUNKS = 4
-FERRIED = ()
-OUTER = ('own', 'reply', 'other', 'weigh', 'far0', 'far1')
-INNER = ('guest0', 'guest1', 'far0', 'lodge', 'weigh', 'far1', 'back0', 'own', 'reply', 'back1')
+OUTER = ('other0', 'own', 'far0', 'reply', 'far1', 'other1', 'weigh')
+INNER = ('guest0', 'own', 'guest1', 'far0', 'lodge', 'far1', 'reply', 'back0', 'weigh', 'back1')
 LIMIT = 56 * 2**20
 
 
@@ -71,7 +70,6 @@
     counts,
     route_out,
     route_in,
-    transit,
     w_sem,
     in_sem,
     out_sem,
@@ -94,8 +92,6 @@
     far_rrecv,
     back_send,
     back_recv,
-    shut_send,
-    shut_recv,
 ):
     me = lax.axis_index("expert")
     group = lax.axis_index("groups")
@@ -119,13 +115,14 @@
     def peer(d):
         return (group, flip(me, d, n))
 
-    each(
-        1,
-        n,
-        lambda d: pl.semaphore_signal(
-            barrier, inc=1, device_id=peer(d), device_id_type=MESH
-        ),
-    )
+    with jax.named_scope('signals'):
+        each(
+            1,
+            n,
+            lambda d: pl.semaphore_signal(
+                barrier, inc=1, device_id=peer(d), device_id_type=MESH
+            ),
+        )
 
     inputs = [
         pltpu.make_async_copy(src, dst, in_sem.at[i])
@@ -142,8 +139,6 @@
         load.start()
     load1 = pltpu.make_async_copy(w1_hbm.at[0], w1, w_sem.at[0])
     load2 = pltpu.make_async_copy(w2_hbm.at[0], w2, w_sem.at[1])
-    load1.start()
-    load2.start()
 
     def remote(src, dst, send, recv, d):
         return pltpu.make_async_remote_copy(
@@ -192,13 +187,13 @@
             mirror,
         )
 
-    def near(side, l):
+    def near(side, l, part=0):
         d = side * lanes + l
         return remote(
             outgoing.at[at(0, d)],
             inbox.at[at(0, d)],
             near_send,
-            near_recv.at[side],
+            near_recv.at[side + part],
             d,
         )
 
@@ -236,23 +231,6 @@
             d,
         )
 
-    def shuttle(g, l, k):
-        return remote(
-            results.at[at((1 + g) * block, l, k)],
-            transit.at[(g,) + at(0, l, k)],
-            shut_send.at[g],
-            shut_recv.at[g, k],
-            l,
-        )
-
-    def ferry(g, l, k):
-        if g == 0:
-            dst, send, recv = returned.at[at(block, l, k)], near_rsend, near_rrecv
-        else:
-            dst = relay_in.at[(g - 1,) + at(block, l, k)]
-            send, recv = far_rsend.at[g - 1], far_rrecv.at[g - 1, k]
-        return remote(transit.at[(g,) + at(0, l, k)], dst, send, recv, lanes)
-
     def back(g, k):
         return remote(
             home_out.at[(g,) + columns(k)],
@@ -273,8 +251,19 @@
             area = inbox.at[(pl.ds(0, count * slot), pl.ds(k * part, part))]
         return pltpu.make_async_copy(area, area, sem)
 
-    for load in inputs:
-        load.wait()
+    def enter():
+        with jax.named_scope('barrier'):
+            pl.semaphore_wait(barrier, n - 1)
+
+    def send_rows():
+        route(1, 2, lanes).start()
+        route(0, 1, half).start()
+        for k in range(chunks):
+            dense(2, lanes, k).start()
+
+    with jax.named_scope('wait_small'):
+        for load in inputs[:3]:
+            load.wait()
     lane = lax.broadcasted_iota(jnp.int32, (1, rows), 1)
     task_id = SHARED * copies + label_ref[...] * task_width + sel_ref[0:1, :] - SHARED
     shared_id = sel_ref[1:2, :] * copies + lane % copies
@@ -310,6 +299,21 @@
     route_out[0] = (far_id ^ relay) * slot + far_rank
     route_out[1] = (near_id ^ flip(me, lanes, n)) * slot + near_rank
 
+    @pl.when(plane == 3)
+    def _():
+        with jax.named_scope('wait_x'):
+            inputs[3].wait()
+        enter()
+        send_rows()
+        load1.start()
+        load2.start()
+
+    @pl.when(plane != 3)
+    def _():
+        inputs[3].wait()
+        load1.start()
+        load2.start()
+
     def choice(slots, count):
         slot_row = lax.broadcasted_iota(jnp.int32, (count, rows), 0)
         return (slot_row == slots).astype(jnp.float32).astype(jnp.bfloat16)
@@ -319,52 +323,51 @@
             jnp.bfloat16
         )
 
-    near_pack = pack(choice(near_slot, span), x_ref[...])
-    outgoing[...] = near_pack
-    inbox[pl.ds(0, slot)] = near_pack[:slot]
-
-    tile = min(1024, hid)
+    with jax.named_scope('near_pack'):
+        near_pack = pack(choice(near_slot, span), x_ref[...])
+        outgoing[...] = near_pack
+        inbox[pl.ds(0, slot)] = near_pack[:slot]
+
+    tile = hid
     out_tile = min(512, width)
 
-    def expand(g):
+    def expand(first, count):
         @pl.loop(0, hid // tile)
         def _(t):
             cols = pl.ds(pl.multiple_of(t * tile, tile), tile)
             h = jnp.dot(
-                inbox[pl.ds(g * block, block)],
+                inbox[pl.ds(first, count)],
                 w1[:, cols],
                 preferred_element_type=jnp.float32,
             )
-            hidden[:, cols] = jax.nn.gelu(h).astype(jnp.bfloat16)
-
-    def shrink(g, cols):
-        y = jnp.dot(hidden[...], w2[:, cols], preferred_element_type=jnp.float32)
-        results[pl.ds(g * block, block), cols] = y.astype(jnp.bfloat16)
-
-    def near_work(g):
-        expand(g)
+            hidden[:count, cols] = jax.nn.gelu(h).astype(jnp.bfloat16)
+
+    def shrink(first, count, cols):
+        y = jnp.dot(
+            hidden[:count], w2[:, cols], preferred_element_type=jnp.float32
+        )
+        results[pl.ds(first, count), cols] = y.astype(jnp.bfloat16)
+
+    def near_work(first, count):
+        expand(first, count)
 
         @pl.loop(0, width // out_tile)
         def _(t):
-            shrink(g, pl.ds(pl.multiple_of(t * out_tile, out_tile), out_tile))
-
-        if g == 0:
+            cols = pl.ds(pl.multiple_of(t * out_tile, out_tile), out_tile)
+            shrink(first, count, cols)
+
+        if first == 0:
             returned[pl.ds(0, slot)] = results[pl.ds(0, slot)]
 
     def far_work(g, send):
         with jax.named_scope(f'far_expand{g}'):
-            expand(2 + g)
+            expand((2 + g) * block, block)
         with jax.named_scope(f'far_shrink{g}'):
-            pair = min(2, chunks)
+            pair = min(4, chunks)
             for j in range(chunks // pair):
-                shrink(2 + g, pl.ds(j * pair * part, pair * part))
+                shrink((2 + g) * block, block, pl.ds(j * pair * part, pair * part))
                 for k in range(j * pair, (j + 1) * pair):
                     send(k)
-
-    def ferry_all(g):
-        for k in range(chunks):
-            bulk(shut_recv.at[g, k], lanes - cross, k).wait()
-            each(cross, lanes, lambda l: ferry(g, l, k).start())
 
     def column(row):
         return jnp.broadcast_to(row, (128, row.shape[1])).T[:, :1]
@@ -403,83 +406,61 @@
         weights[0] = column(jnp.where(task_near, task_weight, shared_weight))
         weights[1] = column(jnp.where(task_near, shared_weight, task_weight))
 
-    with jax.named_scope('barrier'):
-        pl.semaphore_wait(barrier, n - 1)
+    @pl.when(plane != 3)
+    def _():
+        enter()
 
     @pl.when(outer)
     def _():
-        for k in range(chunks):
-            dense(2, lanes, k).start()
-            if k == 0:
-                route(1, 2, lanes).start()
-                route(0, 1, half).start()
+        @pl.when(plane == 0)
+        def _():
+            send_rows()
+
         each(1, lanes, lambda l: near(0, l).start())
         each(1, n, lambda d: tally(d).start())
 
         def own():
             with jax.named_scope('o_wait_own'):
-                load1.wait()
-                load2.wait()
                 bulk(near_recv.at[0], lanes - 1).wait()
             with jax.named_scope('o_work0'):
-                near_work(0)
+                near_work(0, block)
 
         def reply():
             each(1, lanes, lambda d: near_answer(d).start())
 
-        def other():
-            with jax.named_scope('o_wait_other'):
-                bulk(near_recv.at[1], lanes).wait()
-            with jax.named_scope('o_work1'):
-                near_work(1)
-            if 0 in FERRIED:
-                for k in range(chunks):
-                    each(cross, lanes, lambda l: shuttle(0, l, k).start())
-                each(0, cross, lambda l: near_answer(lanes + l).start())
-            else:
-                each(lanes, half, lambda d: near_answer(d).start())
-
-        def await_far(g):
+        def other(lo, hi, part):
+            with jax.named_scope(f'o_wait_other{part}'):
+                bulk(near_recv.at[1 + part], hi - lo).wait()
+            with jax.named_scope(f'o_work1{part}'):
+                near_work(block + lo * slot, (hi - lo) * slot)
+            each(lanes + lo, lanes + hi, lambda d: near_answer(d).start())
+
+        def far_step(g):
+            def send(k):
+                each(0, lanes, lambda l: far_answer(g, 1, l, k).start())
+
             with jax.named_scope(f'o_far_wait{g}'):
                 bulk(far_recv.at[g], lanes).wait()
-
-        def far_step(g):
-            def send(k):
-                if 1 + g in FERRIED:
-                    each(cross, lanes, lambda l: shuttle(1 + g, l, k).start())
-                    each(0, cross, lambda l: far_answer(g, 1, l, k).start())
-                else:
-                    each(0, lanes, lambda l: far_answer(g, 1, l, k).start())
-
             far_work(g, send)
-
-        def carry(g):
-            with jax.named_scope(f'o_ferry{g}'):
-                ferry_all(g)
 
         def weigh_step():
             with jax.named_scope('o_weigh'):
                 weigh()
 
-        steps = {"own": own, "reply": reply, "other": other, "weigh": weigh_step}
+        steps = {"own": own, "reply": reply, "other0": functools.partial(other, 0, cross, 0), "other1": functools.partial(other, cross, lanes, 1), "weigh": weigh_step}
         for g in range(2):
-            steps[f"await{g}"] = functools.partial(await_far, g)
             steps[f"far{g}"] = functools.partial(far_step, g)
-        for g in range(3):
-            steps[f"ferry{g}"] = functools.partial(carry, g)
-        if "await1" not in OUTER:
-            steps["far1"] = lambda: (await_far(1), far_step(1))
-        steps["far0"] = lambda: (await_far(0), far_step(0))
+        load1.wait()
+        load2.wait()
         for step in OUTER:
             steps[step]()
 
     @pl.when(inner)
     def _():
+        route(0, 0, mirror).start()
         for k in range(chunks):
             dense(0, mirror, k).start()
-            if k == 0:
-                route(0, 0, mirror).start()
-        each(0, lanes, lambda l: near(1, l).start())
+        each(0, cross, lambda l: near(1, l).start())
         each(1, lanes, lambda l: near(0, l).start())
         each(1, n, lambda d: tally(d).start())
 
@@ -514,7 +495,7 @@
             with jax.named_scope('i_wait_own'):
                 bulk(near_recv.at[0], lanes - 1).wait()
             with jax.named_scope('i_work0'):
-                near_work(0)
+                near_work(0, block)
 
         def reply():
             each(1, lanes, lambda d: near_answer(d).start())
@@ -527,12 +508,13 @@
                     pass_on(k).wait_recv()
                 with jax.named_scope(f'i_host1_{k}'):
                     host(1, guest_choice, k)
+            each(cross, lanes, lambda l: near(1, l, 1).start())
 
         def lodged():
             with jax.named_scope('i_waitlodge'):
                 bulk(lodge_recv, lanes - 1).wait()
             with jax.named_scope('i_work1'):
-                near_work(1)
+                near_work(block, block)
             each(lanes, half, lambda d: near_answer(d).start())
 
         def take_back(g, lo, hi):
@@ -597,8 +579,6 @@
             bulk(near_send, lanes - 1).wait()
             for g in range(2):
                 bulk(far_rsend.at[g], lanes).wait()
-            for g in FERRIED:
-                bulk(shut_send.at[g], lanes - cross).wait()
 
         @pl.when(inner)
         def _():
@@ -656,7 +636,6 @@
                 pltpu.VMEM((n, 1, padded), f32),
                 pltpu.VMEM((2, 1, rows), i32),
                 pltpu.VMEM((3, 1, rows), i32),
-                pltpu.VMEM((3, lanes * slot, width), bf16),
                 dma((2,)),
                 dma((4,)),
                 dma((chunks,)),
@@ -668,7 +647,7 @@
                 dma(()),
                 dma(()),
                 dma(()),
-                dma((2,)),
+                dma((3,)),
                 dma(()),
                 dma(()),
                 dma((2,)),
@@ -679,8 +658,6 @@
                 dma((2, chunks)),
                 dma(()),
                 dma((chunks,)),
-                dma((3,)),
-                dma((3, chunks)),
             ],
             compiler_params=pltpu.CompilerParams(
                 collective_id=0, has_side_effects=True, vmem_limit_bytes=LIMIT

time: 43.7 us -> 41.9 us (0.959)
  Pallas kernels: 41.8 us -> 40 us
    pallas_call x1, Pallas kernels: 41.8 us -> 40 us  [shards(): pl.pallas_call(functools.partial(kernel, n, slot, chunks), out_shape=jax....]
where the time goes in v2:
time: 41.9 us; the launch traced here: 41.7 us
  Pallas kernels  40 us (95%)
  local copies, waits for them, and re-layouts  1.67 us (4%)
    pallas_call x1, Pallas kernels, shards(): pl.pallas_call(functools.partial(kernel, n, slot, chunks), out_shape=jax....  40 us
    unnamed x1, local copies, waits for them, and re-layouts  1.67 us

profile of v2, /device:TPU:0, one launch (start us, length us, event | category | flops | bytes accessed | tf_op | source)
XLA Modules:
  0.0 41.7 jit_solution(2824015244223732689)
XLA Ops:
  0.0 40.0 %shard_map.73 = bf16[128,1024]{1,0:T(8,128)(2,1)} custom-call(s32[16]{0:T(128)} %room_ref.1, s32[1,128]{1,0:T(1,128)} %bitcast.5, s32[2,128]{1,0:T(2,128)} %bitcast.3, s32[2,128]{1,0:T(2,128)} %bitcast.4, bf16[128,1024]{1,0:T(8,128)(2,1)} %x_hbm.1, bf16[1,1024,2048]{2,1,0:T(8,128)(2,1)} %w1_hbm.1, bf16[1,2048,1024]{2,1,0:T(8,128)(2,1)} %w2_hbm.1), custom_call_target="tpu_custom_call" | custom-call | tf_op jit(solution)/shard_map/pallas_call | solution.py:610
  40.0 1.7 %copy.9 = bf16[128,1024]{1,0:T(8,128)(2,1)} copy(bf16[128,1024]{1,0:T(8,128)(2,1)} %shard_map.73) | data formatting | bytes 524288

commit v3 on v2

--- a/solution.py
+++ b/solution.py
@@ -40,7 +40,7 @@
     n,
     slot,
     chunks,
-    room_ref,
+    room_hbm,
     label_hbm,
     sel_hbm,
     mix_hbm,
@@ -48,6 +48,7 @@
     w1_hbm,
     w2_hbm,
     out_hbm,
+    room_ref,
     label_ref,
     sel_ref,
     mix_ref,
@@ -132,6 +133,7 @@
                 (sel_hbm, sel_ref),
                 (mix_hbm, mix_ref),
                 (x_hbm, x_ref),
+                (room_hbm, room_ref),
             )
         )
     ]
@@ -379,6 +381,7 @@
 
     def weigh():
         pltpu.make_async_copy(counts.at[pl.ds(1, n - 1)], counts.at[pl.ds(1, n - 1)], tally_recv).wait()
+        inputs[4].wait()
         offset = jnp.zeros((1, padded), jnp.float32)
         for d in range(1, n):
             offset = offset + counts[d] * jnp.where(flip(me, d, n) < me, 1.0, 0.0)
@@ -610,10 +613,10 @@
         return pl.pallas_call(
             functools.partial(kernel, n, slot, chunks),
             out_shape=jax.ShapeDtypeStruct((rows, width), bf16),
-            in_specs=[pl.BlockSpec(memory_space=pltpu.SMEM)]
-            + [anywhere] * 6,
+            in_specs=[anywhere] * 7,
             out_specs=anywhere,
             scratch_shapes=[
+                pltpu.SMEM((n,), i32),
                 pltpu.VMEM((1, rows), i32),
                 pltpu.VMEM((2, rows), i32),
                 pltpu.VMEM((2, rows), i32),
@@ -637,7 +640,7 @@
                 pltpu.VMEM((2, 1, rows), i32),
                 pltpu.VMEM((3, 1, rows), i32),
                 dma((2,)),
-                dma((4,)),
+                dma((5,)),
                 dma((chunks,)),
                 dma(()),
                 dma(()),

time: 41.9 us -> 41.1 us (0.981)
  Pallas kernels: 40 us -> 39.3 us
    pallas_call x1, Pallas kernels: 40 us -> 39.3 us  [shards(): pl.pallas_call(functools.partial(kernel, n, slot, chunks), out_shape=jax....]
where the time goes in v3:
time: 41.1 us; the launch traced here: 41 us
  Pallas kernels  39.3 us (96%)
  local copies, waits for them, and re-layouts  1.67 us (4%)
    pallas_call x1, Pallas kernels, shards(): pl.pallas_call(functools.partial(kernel, n, slot, chunks), out_shape=jax....  39.3 us
    unnamed x1, local copies, waits for them, and re-layouts  1.67 us

profile of v3, /device:TPU:0, one launch (start us, length us, event | category | flops | bytes accessed | tf_op | source)
XLA Modules:
  0.0 41.0 jit_solution(14180412235122406945)
XLA Ops:
  0.0 39.3 %shard_map.73 = bf16[128,1024]{1,0:T(8,128)(2,1)} custom-call(s32[16]{0:T(128)} %room_hbm.1, s32[1,128]{1,0:T(1,128)} %bitcast.5, s32[2,128]{1,0:T(2,128)} %bitcast.3, s32[2,128]{1,0:T(2,128)} %bitcast.4, bf16[128,1024]{1,0:T(8,128)(2,1)} %x_hbm.1, bf16[1,1024,2048]{2,1,0:T(8,128)(2,1)} %w1_hbm.1, bf16[1,2048,1024]{2,1,0:T(8,128)(2,1)} %w2_hbm.1), custom_call_target="tpu_custom_call" | custom-call | tf_op jit(solution)/shard_map/pallas_call | solution.py:613
  39.3 1.7 %copy.9 = bf16[128,1024]{1,0:T(8,128)(2,1)} copy(bf16[128,1024]{1,0:T(8,128)(2,1)} %shard_map.73) | data formatting | bytes 524288
